TPU v7x, 256 devices: a whole 4x4x8 slice. The times are simulated.
256 devices in a mesh: gx: 8 (over y, core), gy: 16 (over z, x_lo), gz: 2 (over x_hi).
Axes of the slice: x: 4 (x_hi: 2, x_lo: 2; x = x_hi * 2 + x_lo), y: 4, z: 8, core: 2. Of those that a mesh axis runs over, the one named last changes fastest.
Arguments:
- directions: float32 [8, 128, 256, 256], P(None, 'gx', 'gy', 'gz'), may hold values from -6 to 6
- state: float32 [128, 256, 256], P('gx', 'gy', 'gz'), may hold values from -2 to 2
- log_cond: float32 [128, 256, 256], P('gx', 'gy', 'gz'), may hold values from -1 to 1
- obs_mask: int32 [128, 256, 256], P('gx', 'gy', 'gz'), may hold values 0 or 1
Outputs:
- hessian_action: float32 [8, 128, 256, 256], P(None, 'gx', 'gy', 'gz')
- quotient: float32 [8], replicated
All inputs are finite; a program needn't handle non-finite values. No bound on the sum of `obs_mask` on one device may be relied on, other than what follows from the above.
Results may differ from a plain program's by a relative error of at most 0.00002.
Values sent between devices are 32-bit elements; how exact they have to be, the bound alone decides.
A program may use at most 128 MiB of HBM per device.

v0:
```python
import math

import jax
import jax.numpy as jnp
from jax import lax
from jax.sharding import Mesh
from jax.sharding import PartitionSpec as P

ITERS = 4
GX_GY_GZ = ("gx_0", "gx_1", "gy_0", "gy_1", "gz")
GX = ("gx_0", "gx_1")
GY = ("gy_0", "gy_1")


SHIFT = 0.3
BETA = 0.05
DATA_WEIGHT = 10.0


def with_halo(shard, sides, width):
    for axis, dim in sides:
        size, length = (lax.axis_size(axis), shard.shape[dim])
        up = [(i, (i + 1) % size) for i in range(size - 1)]
        down = [(j, i) for i, j in up]
        last = lax.slice_in_dim(shard, length - width, length, axis=dim)
        leading = lax.slice_in_dim(shard, 0, width, axis=dim)
        before = lax.ppermute(last, axis, up)
        after = lax.ppermute(leading, axis, down)
        shard = jnp.concatenate([before, shard, after], axis=dim)
    return shard


def over_axes(shard, axes):
    for axis in axes:
        shard = lax.psum(shard, axis)
    return shard


def chebyshev(count):
    return [
        1.0 / (1.125 + 0.825 * math.cos(math.pi * (2 * j + 1) / (2 * count))) for j in range(count)
    ]


def neighbours(padded):
    total = padded[..., 2:, 1:-1, 1:-1] + padded[..., :-2, 1:-1, 1:-1]
    total = total + padded[..., 1:-1, 2:, 1:-1] + padded[..., 1:-1, :-2, 1:-1]
    return total + padded[..., 1:-1, 1:-1, 2:] + padded[..., 1:-1, 1:-1, :-2]


def trim_rim(field, layers):
    return field[..., layers:-layers, layers:-layers, layers:-layers]


def trim_to(field, layers):
    if layers == 0:
        return field
    return trim_rim(field, layers)


def shards(directions, state, log_cond, obs_mask):
    cheb_w = chebyshev(ITERS)
    conduct = jnp.exp(log_cond)
    observed = obs_mask.astype(jnp.float32)
    outer = ITERS - 1
    stacked = jnp.concatenate([state[None], conduct[None], directions], axis=0)
    padded = with_halo(stacked, ((GX, 1), (GY, 2), ("gz", 3)), ITERS)
    state_wide = padded[0]
    conduct_wide = trim_rim(padded[1], 1)
    diagonal_wide = SHIFT + 6.0 * conduct_wide
    delta_wide = padded[2:]
    lap_wide = 6.0 * trim_rim(state_wide, 1) - neighbours(state_wide)
    source_wide = -conduct_wide * trim_rim(delta_wide, 1) * lap_wide
    tangent = cheb_w[0] * source_wide / diagonal_wide
    margin = outer
    for step in range(1, ITERS):
        margin = margin - 1
        cut = outer - margin
        inner = trim_rim(tangent, 1)
        cond_here = trim_to(conduct_wide, cut)
        diag_here = trim_to(diagonal_wide, cut)
        applied = diag_here * inner - cond_here * neighbours(tangent)
        tangent = inner + cheb_w[step] * (trim_to(source_wide, cut) - applied) / diag_here
    data_rhs = DATA_WEIGHT * observed * tangent
    rhs_wide = with_halo(data_rhs, ((GX, 1), (GY, 2), ("gz", 3)), outer)
    adjoint = cheb_w[0] * rhs_wide / diagonal_wide
    margin = outer
    for step in range(1, ITERS):
        flux = trim_to(conduct_wide, outer - margin) * adjoint
        margin = margin - 1
        cut = outer - margin
        inner = trim_rim(adjoint, 1)
        diag_here = trim_to(diagonal_wide, cut)
        applied = diag_here * inner - neighbours(flux)
        adjoint = inner + cheb_w[step] * (trim_to(rhs_wide, cut) - applied) / diag_here
    lap_state = trim_to(lap_wide, outer)
    delta_pad = trim_to(delta_wide, outer)
    hessian_action = -conduct * lap_state * adjoint + BETA * (
        6.0 * directions - neighbours(delta_pad)
    )
    cells = (
        directions.shape[1]
        * directions.shape[2]
        * directions.shape[3]
        * lax.axis_size(GX)
        * lax.axis_size(GY)
        * lax.axis_size("gz")
    )
    partial_sums = jnp.sum(directions * hessian_action, axis=(1, 2, 3))
    quotient = over_axes(partial_sums, GX_GY_GZ) / cells
    return (hessian_action, quotient)


def solution(mesh):
    torus = Mesh(
        mesh.devices.reshape(4, 2, 8, 2, mesh.shape["gz"]), ("gx_0", "gx_1", "gy_0", "gy_1", "gz")
    )
    placed = (P(None, GX, GY, "gz"), P(GX, GY, "gz"), P(GX, GY, "gz"), P(GX, GY, "gz"))
    return jax.shard_map(
        shards, mesh=torus, in_specs=placed, out_specs=(P(None, GX, GY, "gz"), P()), check_vma=False
    )
```

profile of v0, /device:TPU:6, one launch (start us, length us, event | category | flops | bytes accessed | tf_op | source)
XLA Modules:
  0.0 247.7 jit_solution(18383695558841984095)
XLA Ops:
  0.6 0.9 exponential_bitcast_fusion
  1.6 1.1 pad_maximum_fusion.30
  2.7 1.9 collective-permute-start
  4.6 1.3 collective-permute-start.1
  6.0 3.5 %collective-permute-done.1 = f32[10,4,16,128]{3,2,1,0:T(8,128)S(1)} collective-permute-done((f32[10,4,16,128]{3,2,1,0:T(8,128)S(1)}, f32[10,4,16,128]{3,2,1,0:T(8,128)S(1)}, u32[]{:S(2)}, u32[]{:S(2)}) %collective-permute-start.1) | collective-permute-done | bytes 327712 | tf_op jit(solution)/shard_map/ppermute | solution.py:28
  9.5 1.5 pad_maximum_fusion.24
  11.1 2.7 %collective-permute-start.3 = (f32[10,24,4,128]{3,1,2,0:T(8,128)S(1)}, f32[10,24,4,128]{3,1,2,0:T(8,128)S(1)}, u32[]{:S(2)}, u32[]{:S(2)}) collective-permute-start(f32[10,24,4,128]{3,1,2,0:T(8,128)S(1)} %copy.40), channel_id=1, source_target_pairs={{2,0},{4,2},{6,4},{8,6},{10,8},{12,10},{14,12},{16,14},{18,16},{20... | collective-permute-start | bytes 1474568 | tf_op jit(solution)/shard_map/ppermute | solution.py:28
  13.9 4.0 %collective-permute-start.2 = (f32[10,24,4,128]{3,1,2,0:T(8,128)S(1)}, f32[10,24,4,128]{3,1,2,0:T(8,128)S(1)}, u32[]{:S(2)}, u32[]{:S(2)}) collective-permute-start(f32[10,24,4,128]{3,1,2,0:T(8,128)S(1)} %copy.39), channel_id=1, source_target_pairs={{0,2},{2,4},{4,6},{6,8},{8,10},{10,12},{12,14},{14,16},{16,18},{18... | collective-permute-start | bytes 1474568 | tf_op jit(solution)/shard_map/ppermute | solution.py:27
  17.9 5.8 %collective-permute-done.3 = f32[10,24,4,128]{3,1,2,0:T(8,128)S(1)} collective-permute-done((f32[10,24,4,128]{3,1,2,0:T(8,128)S(1)}, f32[10,24,4,128]{3,1,2,0:T(8,128)S(1)}, u32[]{:S(2)}, u32[]{:S(2)}) %collective-permute-start.3) | collective-permute-done | bytes 491552 | tf_op jit(solution)/shard_map/ppermute | solution.py:28
  23.7 0.1 copy.42
  23.9 14.6 %collective-permute-done.2 = f32[10,24,4,128]{3,1,2,0:T(8,128)S(1)} collective-permute-done((f32[10,24,4,128]{3,1,2,0:T(8,128)S(1)}, f32[10,24,4,128]{3,1,2,0:T(8,128)S(1)}, u32[]{:S(2)}, u32[]{:S(2)}) %collective-permute-start.2) | collective-permute-done | bytes 491552 | tf_op jit(solution)/shard_map/ppermute | solution.py:27
  38.4 0.1 copy.41
  38.6 0.8 copy-done.8
  39.4 0.5 pad_maximum_fusion.2
  39.9 2.6 %fusion.63 = (f32[10,24,24,4]{3,2,1,0:T(8,128)}, f32[10,24,24,4]{3,2,1,0:T(8,128)S(1)}) fusion(f32[10,24,24,128]{3,2,1,0:T(8,128)S(1)} %pad_maximum_fusion.2), kind=kLoop, calls=%fused_computation.145 | loop fusion | bytes 368640 | tf_op jit(solution)/shard_map/slice | solution.py:26
  42.5 3.7 %copy.44 = f32[10,24,24,4]{2,1,3,0:T(8,128)} copy(f32[10,24,24,4]{3,2,1,0:T(8,128)} %get-tuple-element.17) | data formatting | bytes 184320 | tf_op jit(solution)/shard_map/slice | solution.py:26
  46.2 2.5 %copy.43 = f32[10,24,24,4]{2,1,3,0:T(8,128)} copy(f32[10,24,24,4]{3,2,1,0:T(8,128)S(1)} %get-tuple-element.18) | data formatting | bytes 184320 | tf_op jit(solution)/shard_map/slice | solution.py:25
  48.7 1.3 collective-permute-start.4
  49.9 8.2 %collective-permute-start.5 = (f32[10,24,24,4]{2,1,3,0:T(8,128)}, f32[10,24,24,4]{2,1,3,0:T(8,128)}, u32[]{:S(2)}, u32[]{:S(2)}) collective-permute-start(f32[10,24,24,4]{2,1,3,0:T(8,128)} %copy.44), channel_id=1, source_target_pairs={{1,0},{3,2},{5,4},{7,6},{9,8},{11,10},{13,12},{15,14},{17,16},{19,... | collective-permute-start | bytes 276488 | tf_op jit(solution)/shard_map/ppermute | solution.py:28
  58.1 1.6 convert_multiply_fusion
  59.7 7.9 %collective-permute-done.5 = f32[10,24,24,4]{2,1,3,0:T(8,128)} collective-permute-done((f32[10,24,24,4]{2,1,3,0:T(8,128)}, f32[10,24,24,4]{2,1,3,0:T(8,128)}, u32[]{:S(2)}, u32[]{:S(2)}) %collective-permute-start.5) | collective-permute-done | bytes 92192 | tf_op jit(solution)/shard_map/ppermute | solution.py:28
  67.6 2.5 %copy.46 = f32[10,24,24,4]{3,2,1,0:T(8,128)S(1)} copy(f32[10,24,24,4]{2,1,3,0:T(8,128)} %collective-permute-done.5) | data formatting | bytes 184320 | tf_op jit(solution)/shard_map/ppermute | solution.py:28
  70.1 3.9 %copy.45 = f32[10,24,24,4]{3,2,1,0:T(8,128)} copy(f32[10,24,24,4]{2,1,3,0:T(8,128)} %collective-permute-done.4) | data formatting | bytes 184320 | tf_op jit(solution)/shard_map/ppermute | solution.py:27
  74.0 8.5 %pad_maximum_fusion = f32[10,24,24,136]{3,2,1,0:T(8,128)S(1)} fusion(f32[10,24,24,4]{3,2,1,0:T(8,128)S(1)} %copy.46, f32[10,24,4,128]{3,2,1,0:T(4,128)S(1)} %copy.42, f32[10,4,16,128]{3,2,1,0:T(8,128)} %copy-done.12, f32[8,16,16,128]{3,2,1,0:T(8,128)} %param.4, f32[1,16,16,128]{3,2,1,0:T(8,128)} %copy-done.14, f32[1,16,16,128]{3,2,1,0:T(8,128)} %bitcast.9, ...), kind=kLoop, calls=%fused_computation | loop fusion | flops 6266880 | bytes 6266880 | tf_op jit(solution)/shard_map/concatenate | solution.py:29
  82.6 0.1 slice.399
  82.7 0.2 slice.389
  82.9 0.2 slice.379
  83.1 1.8 fusion.66
  85.1 0.2 slice.388
  85.3 0.2 slice.378
  85.5 1.4 multiply_divide_fusion.1
  87.0 7.5 %fusion.11 = f32[8,20,20,132]{3,2,1,0:T(8,128)S(1)} fusion(f32[8,22,22,134]{3,2,1,0:T(8,128)S(1)} %get-tuple-element.13, f32[8,22,22,134]{3,2,1,0:T(8,128)S(1)} %get-tuple-element.14, f32[20,20,132]{2,1,0:T(8,128)S(1)} %slice.379, f32[20,20,132]{2,1,0:T(8,128)S(1)} %slice.378), kind=kLoop, calls=%fused_computation.26 | loop fusion | flops 5068800 | bytes 15628800 | tf_op jit(solution)/shard_map/add | solution.py:83
  94.5 7.0 %fusion.22 = f32[8,18,18,130]{3,2,1,0:T(8,128)S(1)} fusion(f32[8,20,20,132]{3,2,1,0:T(8,128)S(1)} %fusion.11, f32[8,22,22,134]{3,2,1,0:T(8,128)S(1)} %get-tuple-element.14, f32[18,18,130]{2,1,0:T(8,128)S(1)} %slice.389, f32[18,18,130]{2,1,0:T(8,128)S(1)} %slice.388), kind=kLoop, calls=%fused_computation.47 | loop fusion | flops 4043520 | bytes 12467520 | tf_op jit(solution)/shard_map/add | solution.py:83
  101.5 2.9 %fusion.57 = f32[8,16,16,128]{3,2,1,0:T(8,128)} fusion(f32[8,18,18,130]{3,2,1,0:T(8,128)S(1)} %fusion.22, f32[8,22,22,134]{3,2,1,0:T(8,128)S(1)} %get-tuple-element.14, f32[16,16,128]{2,1,0:T(8,128)S(1)} %slice.399, f32[16,16,128]{2,1,0:T(8,128)S(1)} %slice.398, f32[16,16,128]{2,1,0:T(8,128)S(1)} %copy-done.33), kind=kLoop, calls=%fused_computation.118 | loop fusion | flops 3407872 | bytes 9830400 | tf_op jit(solution)/shard_map/mul | solution.py:84
  104.4 1.1 fusion.65
  105.6 1.3 collective-permute-start.6
  106.9 1.3 collective-permute-start.7
  108.2 7.4 %collective-permute-done.7 = f32[8,3,16,128]{3,2,1,0:T(8,128)S(1)} collective-permute-done((f32[8,3,16,128]{3,2,1,0:T(8,128)S(1)}, f32[8,3,16,128]{3,2,1,0:T(8,128)S(1)}, u32[]{:S(2)}, u32[]{:S(2)}) %collective-permute-start.7) | collective-permute-done | bytes 196640 | tf_op jit(solution)/shard_map/ppermute | solution.py:28
  115.6 1.4 pad_maximum_fusion.27
  117.1 1.9 collective-permute-start.9
  119.1 4.8 %collective-permute-start.8 = (f32[8,22,3,128]{3,0,2,1:T(8,128)S(1)}, f32[8,22,3,128]{3,0,2,1:T(8,128)S(1)}, u32[]{:S(2)}, u32[]{:S(2)}) collective-permute-start(f32[8,22,3,128]{3,0,2,1:T(8,128)S(1)} %copy.47), channel_id=1, source_target_pairs={{0,2},{2,4},{4,6},{6,8},{8,10},{10,12},{12,14},{14,16},{16,18},{18... | collective-permute-start | bytes 811016 | tf_op jit(solution)/shard_map/ppermute | solution.py:27
  123.9 2.5 %collective-permute-done.9 = f32[8,22,3,128]{3,0,2,1:T(8,128)S(1)} collective-permute-done((f32[8,22,3,128]{3,0,2,1:T(8,128)S(1)}, f32[8,22,3,128]{3,0,2,1:T(8,128)S(1)}, u32[]{:S(2)}, u32[]{:S(2)}) %collective-permute-start.9) | collective-permute-done | bytes 270368 | tf_op jit(solution)/shard_map/ppermute | solution.py:28
  126.5 8.2 %collective-permute-done.8 = f32[8,22,3,128]{3,0,2,1:T(8,128)S(1)} collective-permute-done((f32[8,22,3,128]{3,0,2,1:T(8,128)S(1)}, f32[8,22,3,128]{3,0,2,1:T(8,128)S(1)}, u32[]{:S(2)}, u32[]{:S(2)}) %collective-permute-start.8) | collective-permute-done | bytes 270368 | tf_op jit(solution)/shard_map/ppermute | solution.py:27
  134.9 0.7 copy-done.26
  135.6 0.4 pad_maximum_fusion.3
  135.9 2.0 fusion.64
  138.0 1.8 copy.51
  139.8 2.8 %copy.52 = f32[8,22,22,3]{2,0,3,1:T(8,128)S(1)} copy(f32[8,22,22,3]{3,2,1,0:T(8,128)} %get-tuple-element.20) | data formatting | bytes 92928 | tf_op jit(solution)/shard_map/slice | solution.py:26
  142.6 5.9 %collective-permute-start.11 = (f32[8,22,22,3]{2,0,3,1:T(8,128)S(1)}, f32[8,22,22,3]{2,0,3,1:T(8,128)S(1)}, u32[]{:S(2)}, u32[]{:S(2)}) collective-permute-start(f32[8,22,22,3]{2,0,3,1:T(8,128)S(1)} %copy.52), channel_id=1, source_target_pairs={{1,0},{3,2},{5,4},{7,6},{9,8},{11,10},{13,12},{15,14},{17,16},{19,... | collective-permute-start | bytes 139400 | tf_op jit(solution)/shard_map/ppermute | solution.py:28
  148.6 1.3 collective-permute-start.10
  149.9 1.8 slice_multiply_fusion.2
  151.6 8.8 %collective-permute-done.10 = f32[8,22,22,3]{2,0,3,1:T(8,128)S(1)} collective-permute-done((f32[8,22,22,3]{2,0,3,1:T(8,128)}, f32[8,22,22,3]{2,0,3,1:T(8,128)S(1)}, u32[]{:S(2)}, u32[]{:S(2)}) %collective-permute-start.10) | collective-permute-done | bytes 46496 | tf_op jit(solution)/shard_map/ppermute | solution.py:27
  160.4 2.5 %copy.53 = f32[8,22,22,3]{3,2,1,0:T(8,128)} copy(f32[8,22,22,3]{2,0,3,1:T(8,128)S(1)} %collective-permute-done.10) | data formatting | bytes 92928 | tf_op jit(solution)/shard_map/ppermute | solution.py:27
  162.9 2.5 %copy.54 = f32[8,22,22,3]{3,2,1,0:T(8,128)} copy(f32[8,22,22,3]{2,0,3,1:T(8,128)S(1)} %collective-permute-done.11) | data formatting | bytes 92928 | tf_op jit(solution)/shard_map/ppermute | solution.py:28
  165.4 8.1 %broadcast_multiply_fusion = (f32[8,22,22,134]{3,2,1,0:T(8,128)S(1)}, f32[8,22,22,134]{3,2,1,0:T(8,128)}, f32[8,22,22,134]{3,2,1,0:T(8,128)S(1)}) fusion(f32[22,22,134]{2,1,0:T(8,128)} %get-tuple-element.29, f32[22,22,134]{2,1,0:T(8,128)S(1)} %copy-done.5, f32[8,22,22,3]{3,2,1,0:T(8,128)} %copy.54, f32[8,22,3,128]{3,2,1,0:T(4,128)S(1)} %copy-done.25, ...), kind=kLoop, calls=%fused_computation.54 | loop fusion | flops 4669632 | bytes 8820416 | tf_op jit(solution)/shard_map/mul | solution.py:89
  173.5 10.6 %broadcast_multiply_fusion.1 = (f32[8,20,20,132]{3,2,1,0:T(8,128)S(1)}, f32[8,20,20,132]{3,2,1,0:T(8,128)}) fusion(f32[20,20,132]{2,1,0:T(8,128)S(1)} %copy-done.17, f32[8,22,22,134]{3,2,1,0:T(8,128)S(1)} %get-tuple-element.10, f32[20,20,132]{2,1,0:T(8,128)S(1)} %copy-done.19, f32[8,22,22,134]{3,2,1,0:T(8,128)S(1)} %get-tuple-element.12, ...), kind=kLoop, calls=%fused_computation.55 | loop fusion | flops 5068800 | bytes 17318400 | tf_op jit(solution)/shard_map/mul | solution.py:89
  184.2 10.3 %broadcast_multiply_fusion.2 = (f32[8,18,18,130]{3,2,1,0:T(8,128)S(1)}, f32[8,18,18,130]{3,2,1,0:T(8,128)}) fusion(f32[18,18,130]{2,1,0:T(8,128)} %copy-done.20, f32[8,20,20,132]{3,2,1,0:T(8,128)S(1)} %get-tuple-element.8, f32[18,18,130]{2,1,0:T(8,128)} %copy-done.21, f32[8,22,22,134]{3,2,1,0:T(8,128)S(1)} %get-tuple-element.12, ...), kind=kLoop, calls=%fused_computation.56 | loop fusion | flops 4043520 | bytes 13815360 | tf_op jit(solution)/shard_map/mul | solution.py:89
  194.5 7.7 %multiply_reduce_fusion = (f32[8]{0:T(128)S(1)}, f32[8,16,16,128]{3,2,1,0:T(8,128)}) fusion(f32[8,16,16,128]{3,2,1,0:T(8,128)S(1)} %copy-done.3, f32[10,24,4,128]{3,2,1,0:T(4,128)S(1)} %copy-done.7, f32[10,4,16,128]{3,2,1,0:T(8,128)S(1)} %copy-done.13, f32[1,16,16,128]{3,2,1,0:T(8,128)S(1)} %copy-done.15, f32[1,16,16,128]{3,2,1,0:T(8,128)S(1)} %bitcast.11, ...), kind=kLoop, calls=%fused_computation.117 | loop fusion | flops 13893624 | bytes 12832800 | tf_op jit(solution)/shard_map/reduce_sum | solution.py:109
  202.3 11.8 %psum.35 = f32[8]{0:T(128)S(1)} all-reduce(f32[8]{0:T(128)S(1)} %get-tuple-element.4), channel_id=1, replica_groups=mesh['gx_0'=4,'gx_1'=2,'gy_0'=8,'gy_1'=2,'gz'=2] {'gx_0'}, use_global_device_ids=true, to_apply=%region_1.0 | all-reduce | flops 8 | bytes 64 | tf_op jit(solution)/shard_map/psum | solution.py:35
  214.1 2.5 psum.36
  216.5 19.1 %psum.37 = f32[8]{0:T(128)S(1)} all-reduce(f32[8]{0:T(128)S(1)} %psum.36), channel_id=1, replica_groups=mesh['gx_0'=4,'gx_1'=2,'gy_0'=8,'gy_1'=2,'gz'=2] {'gy_0'}, use_global_device_ids=true, to_apply=%region_3.0 | all-reduce | flops 8 | bytes 64 | tf_op jit(solution)/shard_map/psum | solution.py:35
  235.6 4.9 %psum.38 = f32[8]{0:T(128)S(1)} all-reduce(f32[8]{0:T(128)S(1)} %psum.37), channel_id=1, replica_groups=mesh['gx_0'=4,'gx_1'=2,'gy_0'=8,'gy_1'=2,'gz'=2] {'gy_1'}, use_global_device_ids=true, to_apply=%region_4.0 | all-reduce | flops 8 | bytes 64 | tf_op jit(solution)/shard_map/psum | solution.py:35
  240.5 6.4 %psum.39 = f32[8]{0:T(128)S(1)} all-reduce(f32[8]{0:T(128)S(1)} %psum.38), channel_id=1, replica_groups=mesh['gx_0'=4,'gx_1'=2,'gy_0'=8,'gy_1'=2,'gz'=2] {'gz'}, use_global_device_ids=true, to_apply=%region_5.0 | all-reduce | flops 8 | bytes 64 | tf_op jit(solution)/shard_map/psum | solution.py:35
  246.9 0.5 broadcast_multiply_fusion.3
  (78 shorter events, 0.7 us)
Async XLA Ops:
  1.6 37.0 %copy-start.14 = (f32[1,16,16,128]{3,2,1,0:T(8,128)}, f32[1,16,16,128]{3,2,1,0:T(8,128)S(1)}, u32[]{:S(2)}) copy-start(f32[1,16,16,128]{3,2,1,0:T(8,128)S(1)} %exponential_bitcast_fusion) | copy-start | bytes 393220
  2.7 36.7 %copy-start.2 = (f32[8,16,16,128]{3,2,1,0:T(8,128)S(1)}, f32[8,16,16,128]{3,2,1,0:T(8,128)}, u32[]{:S(2)}) copy-start(f32[8,16,16,128]{3,2,1,0:T(8,128)} %param.4) | copy-start | bytes 3145732
  2.7 36.6 %copy-start.22 = (f32[16,16,128]{2,1,0:T(8,128)S(1)}, f32[16,16,128]{2,1,0:T(8,128)}, u32[]{:S(2)}) copy-start(f32[16,16,128]{2,1,0:T(8,128)} %param.5) | copy-start | bytes 393220
  2.7 3.2 %collective-permute-start = (f32[10,4,16,128]{3,2,1,0:T(8,128)S(1)}, f32[10,4,16,128]{3,2,1,0:T(8,128)S(1)}, u32[]{:S(2)}, u32[]{:S(2)}) collective-permute-start(f32[10,4,16,128]{3,2,1,0:T(8,128)S(1)} %get-tuple-element.25), channel_id=1, source_target_pairs={{0,32},{32,64},{64,96},{96,128},{128,160},{160,192},{192,224},{1,3... | collective-permute-start | bytes 983048 | tf_op jit(solution)/shard_map/ppermute | solution.py:27
  4.6 4.9 %collective-permute-start.1 = (f32[10,4,16,128]{3,2,1,0:T(8,128)S(1)}, f32[10,4,16,128]{3,2,1,0:T(8,128)S(1)}, u32[]{:S(2)}, u32[]{:S(2)}) collective-permute-start(f32[10,4,16,128]{3,2,1,0:T(8,128)S(1)} %get-tuple-element.26), channel_id=1, source_target_pairs={{32,0},{64,32},{96,64},{128,96},{160,128},{192,160},{224,192},{33,... | collective-permute-start | bytes 983048 | tf_op jit(solution)/shard_map/ppermute | solution.py:28
  5.9 33.9 %copy-start.10 = (f32[10,4,16,128]{3,2,1,0:T(8,128)}, f32[10,4,16,128]{3,2,1,0:T(8,128)S(1)}, u32[]{:S(2)}) copy-start(f32[10,4,16,128]{3,2,1,0:T(8,128)S(1)} %collective-permute-done) | copy-start | bytes 983044
  9.5 30.4 %copy-start.12 = (f32[10,4,16,128]{3,2,1,0:T(8,128)}, f32[10,4,16,128]{3,2,1,0:T(8,128)S(1)}, u32[]{:S(2)}) copy-start(f32[10,4,16,128]{3,2,1,0:T(8,128)S(1)} %collective-permute-done.1) | copy-start | bytes 983044
  11.1 12.6 %collective-permute-start.3 = (f32[10,24,4,128]{3,1,2,0:T(8,128)S(1)}, f32[10,24,4,128]{3,1,2,0:T(8,128)S(1)}, u32[]{:S(2)}, u32[]{:S(2)}) collective-permute-start(f32[10,24,4,128]{3,1,2,0:T(8,128)S(1)} %copy.40), channel_id=1, source_target_pairs={{2,0},{4,2},{6,4},{8,6},{10,8},{12,10},{14,12},{16,14},{18,16},{20... | collective-permute-start | bytes 1474568 | tf_op jit(solution)/shard_map/ppermute | solution.py:28
  13.9 24.5 %collective-permute-start.2 = (f32[10,24,4,128]{3,1,2,0:T(8,128)S(1)}, f32[10,24,4,128]{3,1,2,0:T(8,128)S(1)}, u32[]{:S(2)}, u32[]{:S(2)}) collective-permute-start(f32[10,24,4,128]{3,1,2,0:T(8,128)S(1)} %copy.39), channel_id=1, source_target_pairs={{0,2},{2,4},{4,6},{6,8},{8,10},{10,12},{12,14},{14,16},{16,18},{18... | collective-permute-start | bytes 1474568 | tf_op jit(solution)/shard_map/ppermute | solution.py:27
  23.9 50.2 %copy-start.6 = (f32[10,24,4,128]{3,2,1,0:T(4,128)}, f32[10,24,4,128]{3,2,1,0:T(4,128)S(1)}, u32[]{:S(2)}) copy-start(f32[10,24,4,128]{3,2,1,0:T(4,128)S(1)} %copy.42) | copy-start | bytes 1474564
  38.6 0.8 copy-start.8
  48.7 21.5 %collective-permute-start.4 = (f32[10,24,24,4]{2,1,3,0:T(8,128)}, f32[10,24,24,4]{2,1,3,0:T(8,128)}, u32[]{:S(2)}, u32[]{:S(2)}) collective-permute-start(f32[10,24,24,4]{2,1,3,0:T(8,128)} %copy.43), channel_id=1, source_target_pairs={{0,1},{2,3},{4,5},{6,7},{8,9},{10,11},{12,13},{14,15},{16,17},{18,... | collective-permute-start | bytes 276488 | tf_op jit(solution)/shard_map/ppermute | solution.py:27
  49.9 17.7 %collective-permute-start.5 = (f32[10,24,24,4]{2,1,3,0:T(8,128)}, f32[10,24,24,4]{2,1,3,0:T(8,128)}, u32[]{:S(2)}, u32[]{:S(2)}) collective-permute-start(f32[10,24,24,4]{2,1,3,0:T(8,128)} %copy.44), channel_id=1, source_target_pairs={{1,0},{3,2},{5,4},{7,6},{9,8},{11,10},{13,12},{15,14},{17,16},{19,... | collective-permute-start | bytes 276488 | tf_op jit(solution)/shard_map/ppermute | solution.py:28
  70.1 12.4 %copy-start.1 = (f32[10,24,24,4]{3,2,1,0:T(8,128)}, f32[10,24,24,4]{3,2,1,0:T(8,128)S(1)}, u32[]{:S(2)}) copy-start(f32[10,24,24,4]{3,2,1,0:T(8,128)S(1)} %copy.46) | copy-start | bytes 276484
  82.9 11.6 %copy-start.20 = (f32[18,18,130]{2,1,0:T(8,128)}, f32[18,18,130]{2,1,0:T(8,128)S(1)}, u32[]{:S(2)}) copy-start(f32[18,18,130]{2,1,0:T(8,128)S(1)} %slice.389) | copy-start | bytes 505444
  83.1 3.9 %copy-start.16 = (f32[20,20,132]{2,1,0:T(8,128)}, f32[20,20,132]{2,1,0:T(8,128)S(1)}, u32[]{:S(2)}) copy-start(f32[20,20,132]{2,1,0:T(8,128)S(1)} %slice.379) | copy-start | bytes 633604
  85.0 2.0 copy-start.4
  85.0 2.0 copy-start.28
  85.1 16.4 %copy-start.30 = (f32[16,16,128]{2,1,0:T(8,128)}, f32[16,16,128]{2,1,0:T(8,128)S(1)}, u32[]{:S(2)}) copy-start(f32[16,16,128]{2,1,0:T(8,128)S(1)} %slice.398) | copy-start | bytes 393220
  85.3 9.2 %copy-start.21 = (f32[18,18,130]{2,1,0:T(8,128)}, f32[18,18,130]{2,1,0:T(8,128)S(1)}, u32[]{:S(2)}) copy-start(f32[18,18,130]{2,1,0:T(8,128)S(1)} %slice.388) | copy-start | bytes 505444
  85.5 1.5 copy-start.18
  94.5 7.0 %copy-start.33 = (f32[16,16,128]{2,1,0:T(8,128)S(1)}, f32[16,16,128]{2,1,0:T(8,128)}, u32[]{:S(2)}) copy-start(f32[16,16,128]{2,1,0:T(8,128)} %convert_multiply_fusion) | copy-start | bytes 393220
  104.4 31.1 %copy-start = (f32[8,16,16,128]{3,2,1,0:T(8,128)S(1)}, f32[8,16,16,128]{3,2,1,0:T(8,128)}, u32[]{:S(2)}) copy-start(f32[8,16,16,128]{3,2,1,0:T(8,128)} %fusion.57) | copy-start | bytes 3145732
  105.6 2.6 %collective-permute-start.6 = (f32[8,3,16,128]{3,2,1,0:T(8,128)S(1)}, f32[8,3,16,128]{3,2,1,0:T(8,128)S(1)}, u32[]{:S(2)}, u32[]{:S(2)}) collective-permute-start(f32[8,3,16,128]{3,2,1,0:T(8,128)S(1)} %get-tuple-element.27), channel_id=1, source_target_pairs={{0,32},{32,64},{64,96},{96,128},{128,160},{160,192},{192,224},{1,3... | collective-permute-start | bytes 589832 | tf_op jit(solution)/shard_map/ppermute | solution.py:27
  106.9 8.7 %collective-permute-start.7 = (f32[8,3,16,128]{3,2,1,0:T(8,128)S(1)}, f32[8,3,16,128]{3,2,1,0:T(8,128)S(1)}, u32[]{:S(2)}, u32[]{:S(2)}) collective-permute-start(f32[8,3,16,128]{3,2,1,0:T(8,128)S(1)} %get-tuple-element.28), channel_id=1, source_target_pairs={{32,0},{64,32},{96,64},{128,96},{160,128},{192,160},{224,192},{33,... | collective-permute-start | bytes 589832 | tf_op jit(solution)/shard_map/ppermute | solution.py:28
  115.6 19.2 %copy-start.29 = (f32[8,3,16,128]{3,2,1,0:T(8,128)}, f32[8,3,16,128]{3,2,1,0:T(8,128)S(1)}, u32[]{:S(2)}) copy-start(f32[8,3,16,128]{3,2,1,0:T(8,128)S(1)} %collective-permute-done.7) | copy-start | bytes 589828
  117.1 9.4 %collective-permute-start.9 = (f32[8,22,3,128]{3,0,2,1:T(8,128)S(1)}, f32[8,22,3,128]{3,0,2,1:T(8,128)S(1)}, u32[]{:S(2)}, u32[]{:S(2)}) collective-permute-start(f32[8,22,3,128]{3,0,2,1:T(8,128)S(1)} %copy.48), channel_id=1, source_target_pairs={{2,0},{4,2},{6,4},{8,6},{10,8},{12,10},{14,12},{16,14},{18,16},{20... | collective-permute-start | bytes 811016 | tf_op jit(solution)/shard_map/ppermute | solution.py:28
  119.1 15.7 %collective-permute-start.8 = (f32[8,22,3,128]{3,0,2,1:T(8,128)S(1)}, f32[8,22,3,128]{3,0,2,1:T(8,128)S(1)}, u32[]{:S(2)}, u32[]{:S(2)}) collective-permute-start(f32[8,22,3,128]{3,0,2,1:T(8,128)S(1)} %copy.47), channel_id=1, source_target_pairs={{0,2},{2,4},{4,6},{6,8},{8,10},{10,12},{12,14},{14,16},{16,18},{18... | collective-permute-start | bytes 811016 | tf_op jit(solution)/shard_map/ppermute | solution.py:27
  126.5 8.3 %copy-start.24 = (f32[8,22,3,128]{3,2,1,0:T(4,128)}, f32[8,22,3,128]{3,2,1,0:T(4,128)S(1)}, u32[]{:S(2)}) copy-start(f32[8,22,3,128]{3,2,1,0:T(4,128)S(1)} %copy.50) | copy-start | bytes 811012
  134.8 0.7 copy-start.26
  139.8 25.6 %copy-start.5 = (f32[22,22,134]{2,1,0:T(8,128)S(1)}, f32[22,22,134]{2,1,0:T(8,128)}, u32[]{:S(2)}) copy-start(f32[22,22,134]{2,1,0:T(8,128)} %copy-done.4) | copy-start | bytes 778276
  139.8 25.6 %copy-start.25 = (f32[8,22,3,128]{3,2,1,0:T(4,128)S(1)}, f32[8,22,3,128]{3,2,1,0:T(4,128)}, u32[]{:S(2)}) copy-start(f32[8,22,3,128]{3,2,1,0:T(4,128)} %copy-done.24) | copy-start | bytes 811012
  139.8 25.6 %copy-start.27 = (f32[8,22,3,128]{3,2,1,0:T(4,128)S(1)}, f32[8,22,3,128]{3,2,1,0:T(4,128)}, u32[]{:S(2)}) copy-start(f32[8,22,3,128]{3,2,1,0:T(4,128)} %copy-done.26) | copy-start | bytes 811012
  142.6 20.2 %collective-permute-start.11 = (f32[8,22,22,3]{2,0,3,1:T(8,128)S(1)}, f32[8,22,22,3]{2,0,3,1:T(8,128)S(1)}, u32[]{:S(2)}, u32[]{:S(2)}) collective-permute-start(f32[8,22,22,3]{2,0,3,1:T(8,128)S(1)} %copy.52), channel_id=1, source_target_pairs={{1,0},{3,2},{5,4},{7,6},{9,8},{11,10},{13,12},{15,14},{17,16},{19,... | collective-permute-start | bytes 139400 | tf_op jit(solution)/shard_map/ppermute | solution.py:28
  148.6 11.8 %collective-permute-start.10 = (f32[8,22,22,3]{2,0,3,1:T(8,128)}, f32[8,22,22,3]{2,0,3,1:T(8,128)S(1)}, u32[]{:S(2)}, u32[]{:S(2)}) collective-permute-start(f32[8,22,22,3]{2,0,3,1:T(8,128)} %copy.51), channel_id=1, source_target_pairs={{0,1},{2,3},{4,5},{6,7},{8,9},{10,11},{12,13},{14,15},{16,17},{18,... | collective-permute-start | bytes 139400 | tf_op jit(solution)/shard_map/ppermute | solution.py:27
  165.4 8.1 %copy-start.17 = (f32[20,20,132]{2,1,0:T(8,128)S(1)}, f32[20,20,132]{2,1,0:T(8,128)}, u32[]{:S(2)}) copy-start(f32[20,20,132]{2,1,0:T(8,128)} %copy-done.16) | copy-start | bytes 633604
  165.4 8.1 %copy-start.19 = (f32[20,20,132]{2,1,0:T(8,128)S(1)}, f32[20,20,132]{2,1,0:T(8,128)}, u32[]{:S(2)}) copy-start(f32[20,20,132]{2,1,0:T(8,128)} %copy-done.18) | copy-start | bytes 633604
  184.1 10.4 %copy-start.3 = (f32[8,16,16,128]{3,2,1,0:T(8,128)S(1)}, f32[8,16,16,128]{3,2,1,0:T(8,128)}, u32[]{:S(2)}) copy-start(f32[8,16,16,128]{3,2,1,0:T(8,128)} %param.4) | copy-start | bytes 3145732
  184.1 10.4 %copy-start.7 = (f32[10,24,4,128]{3,2,1,0:T(4,128)S(1)}, f32[10,24,4,128]{3,2,1,0:T(4,128)}, u32[]{:S(2)}) copy-start(f32[10,24,4,128]{3,2,1,0:T(4,128)} %copy-done.6) | copy-start | bytes 1474564
  184.1 10.4 %copy-start.9 = (f32[10,24,4,128]{3,2,1,0:T(4,128)S(1)}, f32[10,24,4,128]{3,2,1,0:T(4,128)}, u32[]{:S(2)}) copy-start(f32[10,24,4,128]{3,2,1,0:T(4,128)} %copy-done.8) | copy-start | bytes 1474564
  184.1 10.4 %copy-start.11 = (f32[10,4,16,128]{3,2,1,0:T(8,128)S(1)}, f32[10,4,16,128]{3,2,1,0:T(8,128)}, u32[]{:S(2)}) copy-start(f32[10,4,16,128]{3,2,1,0:T(8,128)} %copy-done.10) | copy-start | bytes 983044
  184.1 10.4 %copy-start.13 = (f32[10,4,16,128]{3,2,1,0:T(8,128)S(1)}, f32[10,4,16,128]{3,2,1,0:T(8,128)}, u32[]{:S(2)}) copy-start(f32[10,4,16,128]{3,2,1,0:T(8,128)} %copy-done.12) | copy-start | bytes 983044
  184.1 10.4 %copy-start.15 = (f32[1,16,16,128]{3,2,1,0:T(8,128)S(1)}, f32[1,16,16,128]{3,2,1,0:T(8,128)}, u32[]{:S(2)}) copy-start(f32[1,16,16,128]{3,2,1,0:T(8,128)} %copy-done.14) | copy-start | bytes 393220
  184.2 10.4 %copy-start.23 = (f32[16,16,128]{2,1,0:T(8,128)S(1)}, f32[16,16,128]{2,1,0:T(8,128)}, u32[]{:S(2)}) copy-start(f32[16,16,128]{2,1,0:T(8,128)} %param.5) | copy-start | bytes 393220
  184.2 10.4 %copy-start.31 = (f32[16,16,128]{2,1,0:T(8,128)S(1)}, f32[16,16,128]{2,1,0:T(8,128)}, u32[]{:S(2)}) copy-start(f32[16,16,128]{2,1,0:T(8,128)} %copy-done.30) | copy-start | bytes 393220
  184.2 10.4 %copy-start.32 = (f32[16,16,128]{2,1,0:T(8,128)S(1)}, f32[16,16,128]{2,1,0:T(8,128)}, u32[]{:S(2)}) copy-start(f32[16,16,128]{2,1,0:T(8,128)} %slice_multiply_fusion.2) | copy-start | bytes 393220
where the time goes:
time: 252 us; the launch traced here: 248 us
  other arithmetic  74.6 us (30%)
  waiting for transfers between devices  58.7 us (23%)
  blocking collectives  44.7 us (18%)
  starting transfers between devices  35.9 us (14%)
  local copies, waits for them, and re-layouts  32.2 us (13%)
    psum x5, blocking collectives, over_axes(): shard = lax.psum(shard, axis)  44.7 us
    ppermute x6, waiting for transfers between devices, with_halo(): before = lax.ppermute(last, axis, up)  31.5 us
    mul x3, other arithmetic, shards(): flux = trim_to(conduct_wide, outer - margin) * adjoint  29 us
    ppermute x6, waiting for transfers between devices, with_halo(): after = lax.ppermute(leading, axis, down)  27.2 us
    ppermute x6, starting transfers between devices, with_halo(): after = lax.ppermute(leading, axis, down)  21.3 us
    ppermute x6, starting transfers between devices, with_halo(): before = lax.ppermute(last, axis, up)  14.6 us
    add x2, other arithmetic, shards(): inner + cheb_w[step] * (trim_to(source_wide, cut) - applied) / diag_here  14.4 us
    concatenate x3, other arithmetic, with_halo(): shard = jnp.concatenate([before, shard, after], axis=dim)  9.32 us
  transfers between devices with their start and end apart: 12, of which 8 were waited for; matrix products, arithmetic and copies ran while one was open for 3% of the time, Pallas kernels for 0%

commit v1 on v0

v1 whole, which is shorter than its diff:
```python
import math

import jax
import jax.numpy as jnp
from jax import lax
from jax.experimental import pallas as pl
from jax.experimental.pallas import tpu as pltpu
from jax.sharding import PartitionSpec as P

ITERS = 4
SHIFT = 0.3
BETA = 0.05
DATA_WEIGHT = 10.0

NDIR = 8
EDGE = 16
LANES = 128
DENSE = EDGE * EDGE
PITCH = 24
ROWS = (EDGE + 2) * PITCH
PER = 2
GROUPS = NDIR // PER

DELTA, T1, T2, B0, B1, B2, T0 = range(7)
EXCHANGES = 6
STATE, FIRST = range(2)


def chebyshev(count):
    return [
        1.0 / (1.125 + 0.825 * math.cos(math.pi * (2 * j + 1) / (2 * count))) for j in range(count)
    ]


def dense(x):
    return pl.ds(x * EDGE, EDGE)


def plane(x):
    return pl.ds((x + 1) * PITCH, EDGE)


def row(y):
    return pl.ds(PITCH + y, EDGE, stride=PITCH)


def kernel(
    sizes,
    d_hbm,
    s_hbm,
    c_hbm,
    m_hbm,
    out_hbm,
    quo_ref,
    d_in,
    s_in,
    c_in,
    m_in,
    field,
    y_send,
    y_halo,
    z_send,
    z_halo,
    coef,
    cy_send,
    cy_halo,
    cz_send,
    cz_halo,
    ratio,
    lap,
    weight,
    forcing,
    smooth,
    result,
    partial,
    sum_x,
    sum_y,
    sum_z,
    load_sem,
    dload_sem,
    out_sem,
    send_sem,
    recv_sem,
    csend_sem,
    crecv_sem,
    rsend_sem,
    rrecv_sem,
):
    gx, gy, gz = sizes
    ix, iy, iz = lax.axis_index("gx"), lax.axis_index("gy"), lax.axis_index("gz")
    cheb = chebyshev(ITERS)

    def along_x(o):
        return (lax.rem(ix + o, gx), iy, iz)

    def along_y(o):
        return (ix, lax.rem(iy + o, gy), iz)

    across = (ix, iy, 1 - iz)
    partners = [along_x(o) for o in range(1, gx)] + [along_y(o) for o in range(1, gy)] + [across]

    barrier = pltpu.get_barrier_semaphore()
    for partner in partners:
        pl.semaphore_signal(barrier, inc=1, device_id=partner, device_id_type=pl.DeviceIdType.MESH)

    loads = [
        pltpu.make_async_copy(s_hbm, s_in, load_sem.at[0]),
        pltpu.make_async_copy(c_hbm, c_in, load_sem.at[1]),
        pltpu.make_async_copy(m_hbm, m_in, load_sem.at[2]),
    ]

    def load_group(g):
        dirs = pl.ds(g * PER, PER)
        return pltpu.make_async_copy(d_hbm.at[dirs], d_in.at[dirs], dload_sem.at[g])

    loads[0].start()
    for g in range(GROUPS):
        load_group(g).start()
    loads[1].start()
    loads[2].start()

    targets = [
        (ix - 1, iy, iz),
        (ix + 1, iy, iz),
        (ix, iy - 1, iz),
        (ix, iy + 1, iz),
        across,
    ]
    exists = [ix > 0, ix < gx - 1, iy > 0, iy < gy - 1, None]
    order = (2, 3, 4, 0, 1)

    def where_exists(side):
        return (lambda f: f()) if exists[side] is None else pl.when(exists[side])

    def faces(e, g):
        dirs = pl.ds(g * PER, PER)
        leave = [
            field.at[e, dirs, plane(0)],
            field.at[e, dirs, plane(EDGE - 1)],
            y_send.at[e, 0, dirs],
            y_send.at[e, 1, dirs],
            z_send.at[e, g],
        ]
        arrive = [
            field.at[e, dirs, plane(-1)],
            field.at[e, dirs, plane(EDGE)],
            y_halo.at[e, 0, dirs],
            y_halo.at[e, 1, dirs],
            z_halo.at[e, g],
        ]
        return leave, arrive, send_sem.at[e, g], recv_sem.at[e, g]

    def coef_faces(e):
        leave = [
            coef.at[e, plane(0)],
            coef.at[e, plane(EDGE - 1)],
            cy_send.at[e, 0],
            cy_send.at[e, 1],
            cz_send.at[e],
        ]
        arrive = [
            coef.at[e, plane(-1)],
            coef.at[e, plane(EDGE)],
            cy_halo.at[e, 0],
            cy_halo.at[e, 1],
            cz_halo.at[e],
        ]
        return leave, arrive, csend_sem.at[e], crecv_sem.at[e]

    opposite = (1, 0, 3, 2, 4)

    def outgoing(parts, side):
        leave, arrive, sent, received = parts
        return pltpu.make_async_remote_copy(
            src_ref=leave[side],
            dst_ref=arrive[opposite[side]],
            send_sem=sent.at[side],
            recv_sem=received.at[opposite[side]],
            device_id=targets[side],
            device_id_type=pl.DeviceIdType.MESH,
        )

    def incoming(parts, side):
        leave, arrive, sent, received = parts
        return pltpu.make_async_remote_copy(
            src_ref=leave[side],
            dst_ref=arrive[side],
            send_sem=sent.at[side],
            recv_sem=received.at[side],
            device_id=targets[side],
            device_id_type=pl.DeviceIdType.MESH,
        )

    def send(parts):
        for side in order:

            @where_exists(side)
            def _():
                outgoing(parts, side).start()

    def wait_faces(parts):
        for side in order:

            @where_exists(side)
            def _():
                incoming(parts, side).wait_recv()

    def wait_sent(parts):
        for side in order:

            @where_exists(side)
            def _():
                outgoing(parts, side).wait_send()

    nothing = jnp.zeros((EDGE, LANES), jnp.float32)
    for side in range(4):

        @pl.when(jnp.logical_not(exists[side]))
        def _():
            for e in range(2):
                if side < 2:
                    coef[e, plane(-1 if side == 0 else EDGE), :] = nothing
                else:
                    cy_halo[e, side - 2] = nothing

            @pl.loop(0, EXCHANGES)
            def _(e):
                for dd in range(NDIR):
                    if side < 2:
                        field[e, dd, plane(-1 if side == 0 else EDGE), :] = nothing
                    else:
                        y_halo[e, side - 2, dd] = nothing

    lane = lax.broadcasted_iota(jnp.int32, (EDGE, LANES), 1)
    first_lane, last_lane = lane == 0, lane == LANES - 1
    inner_lane = jnp.where(iz == 0, LANES - 1, 0)
    faces_partner = lane == inner_lane
    lane8 = lax.broadcasted_iota(jnp.int32, (8, LANES), 1)
    slot = lax.rem(lane8 - inner_lane + LANES, LANES)

    def pack(packed, values, place):
        for half in range(2):
            k = place + half
            moved = values[8 * half : 8 * half + 8]
            if k:
                moved = pltpu.roll(moved, k, 1)
            packed = jnp.where(slot == k, moved, packed)
        return packed

    def arrived(packed):
        return jnp.where(iz == 0, pltpu.roll(packed, LANES - 1, 1), pltpu.roll(packed, 1, 1))

    def unpack(packed, place):
        halves = [pltpu.roll(packed, (LANES - place - h) % LANES, 1) for h in range(2)]
        return jnp.concatenate(halves, axis=0)

    def stencil(load, x, packed, place):
        centre = load(0)
        below = jnp.where(first_lane, 0.0, pltpu.roll(centre, 1, 1))
        above = jnp.where(last_lane, 0.0, pltpu.roll(centre, LANES - 1, 1))
        beyond = jnp.where(faces_partner, unpack(packed, place), 0.0)
        total = (load(-PITCH) + load(PITCH)) + (load(-1) + load(1))
        return centre, total + ((below + above) + beyond)

    def field_stencil(e, dd, x, packed, dl):
        def load(offset):
            return field[e, dd, pl.ds((x + 1) * PITCH + offset, EDGE), :]

        return stencil(load, x, packed, dl * 2 * EDGE + 2 * x)

    empty = jnp.zeros((8, LANES), jnp.float32)

    def finish_coef(e, packed):
        cy_send[e, 0] = coef[e, row(0), :]
        cy_send[e, 1] = coef[e, row(EDGE - 1), :]
        cz_send[e] = packed
        send(coef_faces(e))

    def coef_rows(e):
        coef[e, row(-1), :] = cy_halo[e, 0]
        coef[e, row(EDGE), :] = cy_halo[e, 1]

    def finish_dir(e, dd):
        y_send[e, 0, dd] = field[e, dd, row(0), :]
        y_send[e, 1, dd] = field[e, dd, row(EDGE - 1), :]

    def field_rows(e, dd):
        field[e, dd, row(-1), :] = y_halo[e, 0, dd]
        field[e, dd, row(EDGE), :] = y_halo[e, 1, dd]

    loads[0].wait()
    packed = empty
    for x in range(EDGE):
        values = s_in[dense(x), :]
        coef[STATE, plane(x), :] = values
        packed = pack(packed, values, 2 * x)
    pl.semaphore_wait(barrier, len(partners))
    finish_coef(STATE, packed)

    @pl.loop(0, GROUPS)
    def _(g):
        load_group(g).wait()
        packed = empty
        for dl in range(PER):
            dd = g * PER + dl
            for x in range(EDGE):
                values = d_in[dd, dense(x), :]
                field[DELTA, dd, plane(x), :] = values
                packed = pack(packed, values, dl * 2 * EDGE + 2 * x)
            finish_dir(DELTA, dd)
        z_send[DELTA, g] = packed
        send(faces(DELTA, g))

    loads[1].wait()
    for x in range(EDGE):
        conduct = jnp.exp(c_in[dense(x), :])
        ratio[dense(x), :] = conduct / (SHIFT + 6.0 * conduct)
    loads[2].wait()
    for x in range(EDGE):
        weight[dense(x), :] = DATA_WEIGHT * m_in[dense(x), :].astype(jnp.float32)

    wait_faces(coef_faces(STATE))
    coef_rows(STATE)
    state_z = arrived(cz_halo[STATE])
    packed = empty
    for x in range(EDGE):

        def load(offset, x=x):
            return coef[STATE, pl.ds((x + 1) * PITCH + offset, EDGE), :]

        centre, total = stencil(load, x, state_z, 2 * x)
        lap_here = 6.0 * centre - total
        lap[dense(x), :] = lap_here
        first = -cheb[0] * ratio[dense(x), :] * lap_here
        coef[FIRST, plane(x), :] = first
        packed = pack(packed, first, 2 * x)
    finish_coef(FIRST, packed)

    @pl.loop(0, GROUPS)
    def _(g):
        wait_faces(faces(DELTA, g))
        delta_z = arrived(z_halo[DELTA, g])
        for dl in range(PER):
            dd = g * PER + dl
            field_rows(DELTA, dd)
            total = nothing
            for x in range(EDGE):
                centre, near = field_stencil(DELTA, dd, x, delta_z, dl)
                part = BETA * (6.0 * centre - near)
                smooth[dd, dense(x), :] = part
                total = total + centre * part
                forcing[dd, dense(x), :] = -lap[dense(x), :] * centre
                field[T0, dd, plane(x), :] = coef[FIRST, plane(x), :] * centre
            partial[dd] = total[:8] + total[8:]

    def advance(g, src, packed, w, sink):
        carry = empty
        for dl in range(PER):
            dd = g * PER + dl
            carry = sink.begin(dd, carry)
            for x in range(EDGE):
                centre, near = field_stencil(src, dd, x, packed, dl)
                step = ratio[dense(x), :] * (forcing[dd, dense(x), :] + near) - centre
                carry = sink.plane(dd, dl, x, centre + w * step, carry)
            sink.end(dd)
        return carry

    class Iterate:
        def __init__(self, dst):
            self.dst = dst

        def begin(self, dd, carry):
            return carry

        def plane(self, dd, dl, x, values, carry):
            field[self.dst, dd, plane(x), :] = values
            return pack(carry, values, dl * 2 * EDGE + 2 * x)

        def end(self, dd):
            finish_dir(self.dst, dd)

    class Observe(Iterate):
        def begin(self, dd, carry):
            self.total = nothing
            return carry

        def plane(self, dd, dl, x, values, carry):
            rhs = weight[dense(x), :] * values
            forcing[dd, dense(x), :] = rhs
            self.total = self.total + rhs * values
            first = cheb[0] * ratio[dense(x), :] * rhs
            return super().plane(dd, dl, x, first, carry)

        def end(self, dd):
            partial[dd] = partial[dd] + (self.total[:8] + self.total[8:])
            super().end(dd)

    class Result:
        def begin(self, dd, carry):
            return carry

        def plane(self, dd, dl, x, values, carry):
            result[dd, dense(x), :] = smooth[dd, dense(x), :] - lap[dense(x), :] * values
            return carry

        def end(self, dd):
            pass

    def step(src, sink, w):
        @pl.loop(0, GROUPS)
        def _(g):
            wait_faces(faces(src, g))
            for dl in range(PER):
                field_rows(src, g * PER + dl)
            packed = advance(g, src, arrived(z_halo[src, g]), w, sink)
            if isinstance(sink, Iterate):
                z_send[sink.dst, g] = packed
                send(faces(sink.dst, g))
            else:
                store_group(g).start()

    def store_group(g):
        dirs = pl.ds(g * PER, PER)
        return pltpu.make_async_copy(result.at[dirs], out_hbm.at[dirs], out_sem.at[g])

    wait_faces(coef_faces(FIRST))
    first_z = arrived(cz_halo[FIRST])
    repeated = first_z
    for dl in range(1, PER):
        repeated = repeated + pltpu.roll(first_z, dl * 2 * EDGE, 1)

    @pl.loop(0, GROUPS)
    def _(g):
        for dl in range(PER):
            dd = g * PER + dl
            for x in (-1, EDGE):
                field[T0, dd, plane(x), :] = coef[FIRST, plane(x), :] * field[DELTA, dd, plane(x), :]
            field[T0, dd, row(-1), :] = cy_halo[FIRST, 0] * y_halo[DELTA, 0, dd]
            field[T0, dd, row(EDGE), :] = cy_halo[FIRST, 1] * y_halo[DELTA, 1, dd]
        start_z = repeated * arrived(z_halo[DELTA, g])
        z_send[T1, g] = advance(g, T0, start_z, cheb[1], Iterate(T1))
        send(faces(T1, g))

    step(T1, Iterate(T2), cheb[2])
    step(T2, Observe(B0), cheb[3])

    def reduce_start(buf, mine, count, at, base, value):
        buf[mine] = value
        for o in range(1, count):
            pltpu.make_async_remote_copy(
                src_ref=buf.at[mine],
                dst_ref=buf.at[mine],
                send_sem=rsend_sem.at[base + o],
                recv_sem=rrecv_sem.at[base + o],
                device_id=at(o),
                device_id_type=pl.DeviceIdType.MESH,
            ).start()

    def reduce_copy(buf, slot_index, count, at, base, o):
        return pltpu.make_async_remote_copy(
            src_ref=buf.at[slot_index],
            dst_ref=buf.at[slot_index],
            send_sem=rsend_sem.at[base + o],
            recv_sem=rrecv_sem.at[base + o],
            device_id=at(o),
            device_id_type=pl.DeviceIdType.MESH,
        )

    def reduce_end(buf, mine, count, at, base):
        for o in range(1, count):
            reduce_copy(buf, lax.rem(mine + count - o, count), count, at, base, o).wait_recv()
        total = buf[0]
        for i in range(1, count):
            total = total + buf[i]
        return total

    rounds = (
        (sum_x, ix, gx, along_x, 0),
        (sum_y, iy, gy, along_y, gx),
        (sum_z, iz, gz, lambda o: across, gx + gy),
    )

    reduce_start(*rounds[0], jnp.sum(partial[...], axis=1))
    step(B0, Iterate(B1), cheb[1])
    reduce_start(*rounds[1], reduce_end(*rounds[0]))
    step(B1, Iterate(B2), cheb[2])
    reduce_start(*rounds[2], reduce_end(*rounds[1]))
    step(B2, Result(), cheb[3])
    quo_ref[...] = reduce_end(*rounds[2])

    @pl.loop(0, GROUPS)
    def _(g):
        for e in range(EXCHANGES):
            wait_sent(faces(e, g))
        store_group(g).wait()

    for e in range(2):
        wait_sent(coef_faces(e))
    for buf, mine, count, at, base in rounds:
        for o in range(1, count):
            reduce_copy(buf, mine, count, at, base, o).wait_send()


def solution(mesh):
    sizes = tuple(mesh.shape[name] for name in ("gx", "gy", "gz"))
    gx, gy, gz = sizes
    assert gz == 2
    f32 = jnp.float32
    cells = gx * gy * gz * DENSE * LANES

    def shards(directions, state, log_cond, obs_mask):
        assert directions.shape == (NDIR, EDGE, EDGE, LANES)
        any_spec = pl.BlockSpec(memory_space=pl.ANY)
        out, sums = pl.pallas_call(
            lambda *refs: kernel(sizes, *refs),
            out_shape=(
                jax.ShapeDtypeStruct((NDIR, DENSE, LANES), f32),
                jax.ShapeDtypeStruct((NDIR, LANES), f32),
            ),
            in_specs=[any_spec] * 4,
            out_specs=(any_spec, pl.BlockSpec(memory_space=pltpu.VMEM)),
            scratch_shapes=[
                pltpu.VMEM((NDIR, DENSE, LANES), f32),
                pltpu.VMEM((DENSE, LANES), f32),
                pltpu.VMEM((DENSE, LANES), f32),
                pltpu.VMEM((DENSE, LANES), jnp.int32),
                pltpu.VMEM((EXCHANGES + 1, NDIR, ROWS, LANES), f32),
                pltpu.VMEM((EXCHANGES, 2, NDIR, EDGE, LANES), f32),
                pltpu.VMEM((EXCHANGES, 2, NDIR, EDGE, LANES), f32),
                pltpu.VMEM((EXCHANGES, GROUPS, 8, LANES), f32),
                pltpu.VMEM((EXCHANGES, GROUPS, 8, LANES), f32),
                pltpu.VMEM((2, ROWS, LANES), f32),
                pltpu.VMEM((2, 2, EDGE, LANES), f32),
                pltpu.VMEM((2, 2, EDGE, LANES), f32),
                pltpu.VMEM((2, 8, LANES), f32),
                pltpu.VMEM((2, 8, LANES), f32),
                pltpu.VMEM((DENSE, LANES), f32),
                pltpu.VMEM((DENSE, LANES), f32),
                pltpu.VMEM((DENSE, LANES), f32),
                pltpu.VMEM((NDIR, DENSE, LANES), f32),
                pltpu.VMEM((NDIR, DENSE, LANES), f32),
                pltpu.VMEM((NDIR, DENSE, LANES), f32),
                pltpu.VMEM((NDIR, 8, LANES), f32),
                pltpu.VMEM((gx, NDIR, LANES), f32),
                pltpu.VMEM((gy, NDIR, LANES), f32),
                pltpu.VMEM((gz, NDIR, LANES), f32),
                pltpu.SemaphoreType.DMA((3,)),
                pltpu.SemaphoreType.DMA((GROUPS,)),
                pltpu.SemaphoreType.DMA((GROUPS,)),
                pltpu.SemaphoreType.DMA((EXCHANGES, GROUPS, 5)),
                pltpu.SemaphoreType.DMA((EXCHANGES, GROUPS, 5)),
                pltpu.SemaphoreType.DMA((2, 5)),
                pltpu.SemaphoreType.DMA((2, 5)),
                pltpu.SemaphoreType.DMA((gx + gy + gz,)),
                pltpu.SemaphoreType.DMA((gx + gy + gz,)),
            ],
            compiler_params=pltpu.CompilerParams(collective_id=0, has_side_effects=True),
        )(
            directions.reshape(NDIR, DENSE, LANES),
            state.reshape(DENSE, LANES),
            log_cond.reshape(DENSE, LANES),
            obs_mask.reshape(DENSE, LANES),
        )
        return out.reshape(directions.shape), jnp.sum(sums, axis=1) / cells

    placed = P("gx", "gy", "gz")
    stacked = P(None, "gx", "gy", "gz")
    return jax.shard_map(
        shards,
        mesh=mesh,
        in_specs=(stacked, placed, placed, placed),
        out_specs=(stacked, P()),
        check_vma=False,
    )
```

time: 252 us -> 50.2 us (0.20)
  the two profiles are of different devices: /device:TPU:6 before, /device:TPU:8 now
where the time goes in v1:
time: 50.2 us; the launch traced here: 49.7 us
  Pallas kernels  45.5 us (91%)
  local copies, waits for them, and re-layouts  2.94 us (6%)
  between operations  0.65 us (1%)
  other arithmetic  0.63 us (1%)
    pallas_call x1, Pallas kernels, shards(): pl.pallas_call(lambda *refs: kernel(sizes, *refs), out_shape=(jax.ShapeDt...  45.5 us
    unnamed x3, local copies, waits for them, and re-layouts  2.94 us

profile of v1, /device:TPU:8, one launch (start us, length us, event | category | flops | bytes accessed | tf_op | source)
XLA Modules:
  0.0 49.7 jit_solution(6453481302460220411)
XLA Ops:
  0.6 45.5 %shard_map.59 = (f32[8,256,128]{2,1,0:T(8,128)}, f32[8,128]{1,0:T(8,128)}) custom-call(f32[8,256,128]{2,1,0:T(8,128)} %bitcast.5, f32[256,128]{1,0:T(8,128)} %bitcast.7, f32[256,128]{1,0:T(8,128)} %bitcast.8, s32[256,128]{1,0:T(8,128)} %bitcast.9), custom_call_target="tpu_custom_call" | custom-call | tf_op jit(solution)/shard_map/pallas_call | solution.py:514
  46.1 0.0 copy-start
  46.1 0.7 %copy-done = f32[8,128]{1,0:T(8,128)S(1)} copy-done((f32[8,128]{1,0:T(8,128)S(1)}, f32[8,128]{1,0:T(8,128)}, u32[]{:S(2)}) %copy-start) | copy-done | bytes 4120
  46.8 0.1 reduce_sum.9
  46.9 0.5 %broadcast_multiply_fusion = f32[8]{0:T(128)} fusion(f32[8]{0:T(128)S(1)} %reduce_sum.9), kind=kLoop, calls=%fused_computation | loop fusion | flops 8 | bytes 64 | tf_op jit(solution)/shard_map/div | solution.py:564
  47.4 2.3 %copy.7 = f32[8,16,16,128]{3,2,1,0:T(8,128)} copy(f32[8,16,16,128]{3,2,1,0:T(8,128)} %bitcast.6) | data formatting | bytes 2097152
Async XLA Ops:
  46.1 0.7 %copy-start = (f32[8,128]{1,0:T(8,128)S(1)}, f32[8,128]{1,0:T(8,128)}, u32[]{:S(2)}) copy-start(f32[8,128]{1,0:T(8,128)} %get-tuple-element.5) | copy-start | bytes 12292

commit v2 on v1

--- a/solution.py
+++ b/solution.py
@@ -24,6 +24,7 @@
 DELTA, T1, T2, B0, B1, B2, T0 = range(7)
 EXCHANGES = 6
 STATE, FIRST = range(2)
+GREETED = (0, 1, 2)
 
 
 def chebyshev(count):
@@ -50,7 +51,7 @@
     s_hbm,
     c_hbm,
     m_hbm,
-    out_hbm,
+    result,
     quo_ref,
     d_in,
     s_in,
@@ -71,14 +72,10 @@
     weight,
     forcing,
     smooth,
-    result,
     partial,
-    sum_x,
-    sum_y,
-    sum_z,
+    sums,
     load_sem,
     dload_sem,
-    out_sem,
     send_sem,
     recv_sem,
     csend_sem,
@@ -90,35 +87,7 @@
     ix, iy, iz = lax.axis_index("gx"), lax.axis_index("gy"), lax.axis_index("gz")
     cheb = chebyshev(ITERS)
 
-    def along_x(o):
-        return (lax.rem(ix + o, gx), iy, iz)
-
-    def along_y(o):
-        return (ix, lax.rem(iy + o, gy), iz)
-
     across = (ix, iy, 1 - iz)
-    partners = [along_x(o) for o in range(1, gx)] + [along_y(o) for o in range(1, gy)] + [across]
-
-    barrier = pltpu.get_barrier_semaphore()
-    for partner in partners:
-        pl.semaphore_signal(barrier, inc=1, device_id=partner, device_id_type=pl.DeviceIdType.MESH)
-
-    loads = [
-        pltpu.make_async_copy(s_hbm, s_in, load_sem.at[0]),
-        pltpu.make_async_copy(c_hbm, c_in, load_sem.at[1]),
-        pltpu.make_async_copy(m_hbm, m_in, load_sem.at[2]),
-    ]
-
-    def load_group(g):
-        dirs = pl.ds(g * PER, PER)
-        return pltpu.make_async_copy(d_hbm.at[dirs], d_in.at[dirs], dload_sem.at[g])
-
-    loads[0].start()
-    for g in range(GROUPS):
-        load_group(g).start()
-    loads[1].start()
-    loads[2].start()
-
     targets = [
         (ix - 1, iy, iz),
         (ix + 1, iy, iz),
@@ -131,6 +100,53 @@
 
     def where_exists(side):
         return (lambda f: f()) if exists[side] is None else pl.when(exists[side])
+
+    counts = (8, 8, 4)
+    places = (
+        2 * lax.rem(ix, 4) + lax.rem(iy // 2, 2),
+        4 * (ix // 4) + 2 * iz + lax.rem(iy, 2),
+        iy // 4,
+    )
+
+    def peer(stage, o):
+        other = lax.rem(places[stage] + o, counts[stage])
+        return (
+            (4 * (ix // 4) + other // 2, 4 * (iy // 4) + 2 * lax.rem(other, 2) + lax.rem(iy, 2), iz),
+            (
+                4 * (other // 4) + lax.rem(ix, 4),
+                2 * (iy // 2) + lax.rem(other, 2),
+                lax.rem(other // 2, 2),
+            ),
+            (ix, 4 * other + lax.rem(iy, 4), iz),
+        )[stage]
+
+    barrier = pltpu.get_barrier_semaphore()
+
+    def greet(device):
+        pl.semaphore_signal(barrier, inc=1, device_id=device, device_id_type=pl.DeviceIdType.MESH)
+
+    for stage in GREETED:
+        for o in range(1, counts[stage]):
+            greet(peer(stage, o))
+    for side in range(5):
+        where_exists(side)(lambda: greet(targets[side]))
+    greeted = 1 + sum(counts[stage] - 1 for stage in GREETED) + sum(jnp.where(here, 1, 0) for here in exists[:4])
+
+    loads = [
+        pltpu.make_async_copy(s_hbm, s_in, load_sem.at[0]),
+        pltpu.make_async_copy(c_hbm, c_in, load_sem.at[1]),
+        pltpu.make_async_copy(m_hbm, m_in, load_sem.at[2]),
+    ]
+
+    def load_group(g):
+        dirs = pl.ds(g * PER, PER)
+        return pltpu.make_async_copy(d_hbm.at[dirs], d_in.at[dirs], dload_sem.at[g])
+
+    loads[0].start()
+    for g in range(GROUPS):
+        load_group(g).start()
+    loads[1].start()
+    loads[2].start()
 
     def faces(e, g):
         dirs = pl.ds(g * PER, PER)
@@ -191,8 +207,8 @@
             device_id_type=pl.DeviceIdType.MESH,
         )
 
-    def send(parts):
-        for side in order:
+    def send(parts, sides=order):
+        for side in sides:
 
             @where_exists(side)
             def _():
@@ -294,7 +310,7 @@
         values = s_in[dense(x), :]
         coef[STATE, plane(x), :] = values
         packed = pack(packed, values, 2 * x)
-    pl.semaphore_wait(barrier, len(partners))
+    pl.semaphore_wait(barrier, greeted)
     finish_coef(STATE, packed)
 
     @pl.loop(0, GROUPS)
@@ -354,56 +370,65 @@
             partial[dd] = total[:8] + total[8:]
 
     def advance(g, src, packed, w, sink):
-        carry = empty
         for dl in range(PER):
             dd = g * PER + dl
-            carry = sink.begin(dd, carry)
+            sink.begin()
             for x in range(EDGE):
                 centre, near = field_stencil(src, dd, x, packed, dl)
                 step = ratio[dense(x), :] * (forcing[dd, dense(x), :] + near) - centre
-                carry = sink.plane(dd, dl, x, centre + w * step, carry)
+                sink.plane(dd, x, centre + w * step)
             sink.end(dd)
-        return carry
+        sink.leave(g)
 
     class Iterate:
         def __init__(self, dst):
             self.dst = dst
 
-        def begin(self, dd, carry):
-            return carry
-
-        def plane(self, dd, dl, x, values, carry):
+        def begin(self):
+            pass
+
+        def plane(self, dd, x, values):
             field[self.dst, dd, plane(x), :] = values
-            return pack(carry, values, dl * 2 * EDGE + 2 * x)
 
         def end(self, dd):
             finish_dir(self.dst, dd)
 
+        def leave(self, g):
+            parts = faces(self.dst, g)
+            send(parts, (2, 3, 0, 1))
+            packed = empty
+            for dl in range(PER):
+                for x in range(EDGE):
+                    values = field[self.dst, g * PER + dl, plane(x), :]
+                    packed = pack(packed, values, dl * 2 * EDGE + 2 * x)
+            z_send[self.dst, g] = packed
+            send(parts, (4,))
+
     class Observe(Iterate):
-        def begin(self, dd, carry):
+        def begin(self):
             self.total = nothing
-            return carry
-
-        def plane(self, dd, dl, x, values, carry):
+
+        def plane(self, dd, x, values):
             rhs = weight[dense(x), :] * values
             forcing[dd, dense(x), :] = rhs
             self.total = self.total + rhs * values
-            first = cheb[0] * ratio[dense(x), :] * rhs
-            return super().plane(dd, dl, x, first, carry)
+            super().plane(dd, x, cheb[0] * ratio[dense(x), :] * rhs)
 
         def end(self, dd):
             partial[dd] = partial[dd] + (self.total[:8] + self.total[8:])
             super().end(dd)
 
-    class Result:
-        def begin(self, dd, carry):
-            return carry
-
-        def plane(self, dd, dl, x, values, carry):
+    class Result(Iterate):
+        def __init__(self):
+            pass
+
+        def plane(self, dd, x, values):
             result[dd, dense(x), :] = smooth[dd, dense(x), :] - lap[dense(x), :] * values
-            return carry
 
         def end(self, dd):
+            pass
+
+        def leave(self, g):
             pass
 
     def step(src, sink, w):
@@ -412,16 +437,7 @@
             wait_faces(faces(src, g))
             for dl in range(PER):
                 field_rows(src, g * PER + dl)
-            packed = advance(g, src, arrived(z_halo[src, g]), w, sink)
-            if isinstance(sink, Iterate):
-                z_send[sink.dst, g] = packed
-                send(faces(sink.dst, g))
-            else:
-                store_group(g).start()
-
-    def store_group(g):
-        dirs = pl.ds(g * PER, PER)
-        return pltpu.make_async_copy(result.at[dirs], out_hbm.at[dirs], out_sem.at[g])
+            advance(g, src, arrived(z_halo[src, g]), w, sink)
 
     wait_faces(coef_faces(FIRST))
     first_z = arrived(cz_halo[FIRST])
@@ -438,87 +454,77 @@
             field[T0, dd, row(-1), :] = cy_halo[FIRST, 0] * y_halo[DELTA, 0, dd]
             field[T0, dd, row(EDGE), :] = cy_halo[FIRST, 1] * y_halo[DELTA, 1, dd]
         start_z = repeated * arrived(z_halo[DELTA, g])
-        z_send[T1, g] = advance(g, T0, start_z, cheb[1], Iterate(T1))
-        send(faces(T1, g))
+        advance(g, T0, start_z, cheb[1], Iterate(T1))
 
     step(T1, Iterate(T2), cheb[2])
     step(T2, Observe(B0), cheb[3])
 
-    def reduce_start(buf, mine, count, at, base, value):
-        buf[mine] = value
-        for o in range(1, count):
-            pltpu.make_async_remote_copy(
-                src_ref=buf.at[mine],
-                dst_ref=buf.at[mine],
-                send_sem=rsend_sem.at[base + o],
-                recv_sem=rrecv_sem.at[base + o],
-                device_id=at(o),
-                device_id_type=pl.DeviceIdType.MESH,
-            ).start()
-
-    def reduce_copy(buf, slot_index, count, at, base, o):
+    def sum_copy(stage, place, o):
         return pltpu.make_async_remote_copy(
-            src_ref=buf.at[slot_index],
-            dst_ref=buf.at[slot_index],
-            send_sem=rsend_sem.at[base + o],
-            recv_sem=rrecv_sem.at[base + o],
-            device_id=at(o),
+            src_ref=sums.at[stage, place],
+            dst_ref=sums.at[stage, place],
+            send_sem=rsend_sem.at[stage, o],
+            recv_sem=rrecv_sem.at[stage, o],
+            device_id=peer(stage, o),
             device_id_type=pl.DeviceIdType.MESH,
         )
 
-    def reduce_end(buf, mine, count, at, base):
-        for o in range(1, count):
-            reduce_copy(buf, lax.rem(mine + count - o, count), count, at, base, o).wait_recv()
-        total = buf[0]
-        for i in range(1, count):
-            total = total + buf[i]
-        return total
-
-    rounds = (
-        (sum_x, ix, gx, along_x, 0),
-        (sum_y, iy, gy, along_y, gx),
-        (sum_z, iz, gz, lambda o: across, gx + gy),
-    )
-
-    reduce_start(*rounds[0], jnp.sum(partial[...], axis=1))
+    def sum_start(stage, value):
+        sums[stage, places[stage]] = value
+        for o in range(1, counts[stage]):
+            sum_copy(stage, places[stage], o).start()
+
+    def sum_end(stage):
+        for o in range(1, counts[stage]):
+            sum_copy(stage, lax.rem(places[stage] + counts[stage] - o, counts[stage]), o).wait_recv()
+        parts = [sums[stage, place] for place in range(counts[stage])]
+        while len(parts) > 1:
+            parts = [p + q for p, q in zip(parts[::2], parts[1::2])]
+        return parts[0]
+
+    sum_start(0, jnp.sum(partial[...], axis=1))
     step(B0, Iterate(B1), cheb[1])
-    reduce_start(*rounds[1], reduce_end(*rounds[0]))
+    sum_start(1, sum_end(0))
     step(B1, Iterate(B2), cheb[2])
-    reduce_start(*rounds[2], reduce_end(*rounds[1]))
+    sum_start(2, sum_end(1))
     step(B2, Result(), cheb[3])
-    quo_ref[...] = reduce_end(*rounds[2])
+    quo_ref[...] = sum_end(2)
 
     @pl.loop(0, GROUPS)
     def _(g):
         for e in range(EXCHANGES):
             wait_sent(faces(e, g))
-        store_group(g).wait()
 
     for e in range(2):
         wait_sent(coef_faces(e))
-    for buf, mine, count, at, base in rounds:
-        for o in range(1, count):
-            reduce_copy(buf, mine, count, at, base, o).wait_send()
+    for stage in range(3):
+        for o in range(1, counts[stage]):
+            sum_copy(stage, places[stage], o).wait_send()
+
+
+def finish(cells, sums, quo_ref):
+    quo_ref[...] = jnp.sum(sums[...], axis=1) / cells
 
 
 def solution(mesh):
     sizes = tuple(mesh.shape[name] for name in ("gx", "gy", "gz"))
     gx, gy, gz = sizes
-    assert gz == 2
+    assert sizes == (8, 16, 2)
     f32 = jnp.float32
     cells = gx * gy * gz * DENSE * LANES
 
     def shards(directions, state, log_cond, obs_mask):
         assert directions.shape == (NDIR, EDGE, EDGE, LANES)
         any_spec = pl.BlockSpec(memory_space=pl.ANY)
-        out, sums = pl.pallas_call(
+        vmem_spec = pl.BlockSpec(memory_space=pltpu.VMEM)
+        result, sums = pl.pallas_call(
             lambda *refs: kernel(sizes, *refs),
             out_shape=(
-                jax.ShapeDtypeStruct((NDIR, DENSE, LANES), f32),
-                jax.ShapeDtypeStruct((NDIR, LANES), f32),
+                pltpu.VMEM((NDIR, DENSE, LANES), f32),
+                pltpu.VMEM((NDIR, LANES), f32),
             ),
             in_specs=[any_spec] * 4,
-            out_specs=(any_spec, pl.BlockSpec(memory_space=pltpu.VMEM)),
+            out_specs=(vmem_spec, vmem_spec),
             scratch_shapes=[
                 pltpu.VMEM((NDIR, DENSE, LANES), f32),
                 pltpu.VMEM((DENSE, LANES), f32),
@@ -539,20 +545,16 @@
                 pltpu.VMEM((DENSE, LANES), f32),
                 pltpu.VMEM((NDIR, DENSE, LANES), f32),
                 pltpu.VMEM((NDIR, DENSE, LANES), f32),
-                pltpu.VMEM((NDIR, DENSE, LANES), f32),
                 pltpu.VMEM((NDIR, 8, LANES), f32),
-                pltpu.VMEM((gx, NDIR, LANES), f32),
-                pltpu.VMEM((gy, NDIR, LANES), f32),
-                pltpu.VMEM((gz, NDIR, LANES), f32),
+                pltpu.VMEM((3, 8, NDIR, LANES), f32),
                 pltpu.SemaphoreType.DMA((3,)),
-                pltpu.SemaphoreType.DMA((GROUPS,)),
                 pltpu.SemaphoreType.DMA((GROUPS,)),
                 pltpu.SemaphoreType.DMA((EXCHANGES, GROUPS, 5)),
                 pltpu.SemaphoreType.DMA((EXCHANGES, GROUPS, 5)),
                 pltpu.SemaphoreType.DMA((2, 5)),
                 pltpu.SemaphoreType.DMA((2, 5)),
-                pltpu.SemaphoreType.DMA((gx + gy + gz,)),
-                pltpu.SemaphoreType.DMA((gx + gy + gz,)),
+                pltpu.SemaphoreType.DMA((3, 8)),
+                pltpu.SemaphoreType.DMA((3, 8)),
             ],
             compiler_params=pltpu.CompilerParams(collective_id=0, has_side_effects=True),
         )(
@@ -561,7 +563,13 @@
             log_cond.reshape(DENSE, LANES),
             obs_mask.reshape(DENSE, LANES),
         )
-        return out.reshape(directions.shape), jnp.sum(sums, axis=1) / cells
+        quotient = pl.pallas_call(
+            lambda *refs: finish(cells, *refs),
+            out_shape=jax.ShapeDtypeStruct((NDIR,), f32),
+            in_specs=[vmem_spec],
+            out_specs=vmem_spec,
+        )(pltpu.with_memory_space_constraint(sums, pltpu.VMEM))
+        return result.reshape(directions.shape), quotient
 
     placed = P("gx", "gy", "gz")
     stacked = P(None, "gx", "gy", "gz")

time: 50.2 us -> 48.2 us (0.960)
  local copies, waits for them, and re-layouts: 2.94 us -> 0.97 us
  Pallas kernels: 45.5 us -> 46.5 us
  other arithmetic: 0.63 us -> 0 us
    unnamed x3 -> x1, local copies, waits for them, and re-layouts: 2.94 us -> 0.97 us
    pallas_call x1 -> x2, Pallas kernels: 45.5 us -> 46.5 us  [the longest x1 45.9 us: shards(): pl.pallas_call(lambda *refs: kernel(sizes, *refs), out_shape=(pltpu.VMEM(...]
    div x1 -> x0, other arithmetic: 0.52 us -> none  [shards(): return (out.reshape(directions.shape), jnp.sum(sums, axis=1) / cells)]
where the time goes in v2:
time: 48.2 us; the launch traced here: 48.1 us
  Pallas kernels  46.5 us (96%)
  local copies, waits for them, and re-layouts  0.97 us (2%)
  between operations  0.64 us (1%)
    pallas_call x1, Pallas kernels, shards(): pl.pallas_call(lambda *refs: kernel(sizes, *refs), out_shape=(pltpu.VMEM(...  45.9 us
    unnamed x1, local copies, waits for them, and re-layouts  0.97 us

profile of v2, /device:TPU:8, one launch (start us, length us, event | category | flops | bytes accessed | tf_op | source)
XLA Modules:
  0.0 48.1 jit_solution(9703000493953610616)
XLA Ops:
  0.6 45.9 %shard_map.59 = (f32[8,256,128]{2,1,0:T(8,128)S(1)}, f32[8,128]{1,0:T(8,128)S(1)}) custom-call(f32[8,256,128]{2,1,0:T(8,128)} %bitcast.6, f32[256,128]{1,0:T(8,128)} %bitcast.7, f32[256,128]{1,0:T(8,128)} %bitcast.8, s32[256,128]{1,0:T(8,128)} %bitcast.9), custom_call_target="tpu_custom_call" | custom-call | tf_op jit(solution)/shard_map/pallas_call | solution.py:520
  46.6 1.0 %copy.7 = f32[8,16,16,128]{3,2,1,0:T(8,128)} copy(f32[8,16,16,128]{3,2,1,0:T(8,128)S(1)} %bitcast.5) | data formatting | bytes 2097152
  47.6 0.6 %shard_map.60 = f32[8]{0:T(128)} custom-call(f32[8,128]{1,0:T(8,128)S(1)} %get-tuple-element.5.refs_0_), custom_call_target="tpu_custom_call" | custom-call | tf_op jit(solution)/shard_map/pallas_call | solution.py:566

commit v3 on v2

--- a/solution.py
+++ b/solution.py
@@ -101,24 +101,40 @@
     def where_exists(side):
         return (lambda f: f()) if exists[side] is None else pl.when(exists[side])
 
-    counts = (8, 8, 4)
+    counts = (8, 4, 8)
     places = (
         2 * lax.rem(ix, 4) + lax.rem(iy // 2, 2),
+        iy // 4,
         4 * (ix // 4) + 2 * iz + lax.rem(iy, 2),
-        iy // 4,
     )
 
     def peer(stage, o):
         other = lax.rem(places[stage] + o, counts[stage])
         return (
             (4 * (ix // 4) + other // 2, 4 * (iy // 4) + 2 * lax.rem(other, 2) + lax.rem(iy, 2), iz),
+            (ix, 4 * other + lax.rem(iy, 4), iz),
             (
                 4 * (other // 4) + lax.rem(ix, 4),
                 2 * (iy // 2) + lax.rem(other, 2),
                 lax.rem(other // 2, 2),
             ),
-            (ix, 4 * other + lax.rem(iy, 4), iz),
         )[stage]
+
+    loads = [
+        pltpu.make_async_copy(s_hbm, s_in, load_sem.at[0]),
+        pltpu.make_async_copy(c_hbm, c_in, load_sem.at[1]),
+        pltpu.make_async_copy(m_hbm, m_in, load_sem.at[2]),
+    ]
+
+    def load_group(g):
+        dirs = pl.ds(g * PER, PER)
+        return pltpu.make_async_copy(d_hbm.at[dirs], d_in.at[dirs], dload_sem.at[g])
+
+    loads[0].start()
+    for g in range(GROUPS):
+        load_group(g).start()
+    loads[1].start()
+    loads[2].start()
 
     barrier = pltpu.get_barrier_semaphore()
 
@@ -131,22 +147,6 @@
     for side in range(5):
         where_exists(side)(lambda: greet(targets[side]))
     greeted = 1 + sum(counts[stage] - 1 for stage in GREETED) + sum(jnp.where(here, 1, 0) for here in exists[:4])
-
-    loads = [
-        pltpu.make_async_copy(s_hbm, s_in, load_sem.at[0]),
-        pltpu.make_async_copy(c_hbm, c_in, load_sem.at[1]),
-        pltpu.make_async_copy(m_hbm, m_in, load_sem.at[2]),
-    ]
-
-    def load_group(g):
-        dirs = pl.ds(g * PER, PER)
-        return pltpu.make_async_copy(d_hbm.at[dirs], d_in.at[dirs], dload_sem.at[g])
-
-    loads[0].start()
-    for g in range(GROUPS):
-        load_group(g).start()
-    loads[1].start()
-    loads[2].start()
 
     def faces(e, g):
         dirs = pl.ds(g * PER, PER)
@@ -369,6 +369,29 @@
                 field[T0, dd, plane(x), :] = coef[FIRST, plane(x), :] * centre
             partial[dd] = total[:8] + total[8:]
 
+    def sum_copy(stage, place, o):
+        return pltpu.make_async_remote_copy(
+            src_ref=sums.at[stage, place],
+            dst_ref=sums.at[stage, place],
+            send_sem=rsend_sem.at[stage, o],
+            recv_sem=rrecv_sem.at[stage, o],
+            device_id=peer(stage, o),
+            device_id_type=pl.DeviceIdType.MESH,
+        )
+
+    def sum_start(stage, value):
+        sums[stage, places[stage]] = value
+        for o in range(1, counts[stage]):
+            sum_copy(stage, places[stage], o).start()
+
+    def sum_end(stage):
+        for o in range(1, counts[stage]):
+            sum_copy(stage, lax.rem(places[stage] + counts[stage] - o, counts[stage]), o).wait_recv()
+        parts = [sums[stage, place] for place in range(counts[stage])]
+        while len(parts) > 1:
+            parts = [p + q for p, q in zip(parts[::2], parts[1::2])]
+        return parts[0]
+
     def advance(g, src, packed, w, sink):
         for dl in range(PER):
             dd = g * PER + dl
@@ -418,6 +441,13 @@
             partial[dd] = partial[dd] + (self.total[:8] + self.total[8:])
             super().end(dd)
 
+        def leave(self, g):
+            @pl.when(g == GROUPS - 1)
+            def _():
+                sum_start(0, jnp.sum(partial[...], axis=1))
+
+            super().leave(g)
+
     class Result(Iterate):
         def __init__(self):
             pass
@@ -431,13 +461,15 @@
         def leave(self, g):
             pass
 
-    def step(src, sink, w):
+    def step(src, sink, w, after=None, then=None):
         @pl.loop(0, GROUPS)
         def _(g):
             wait_faces(faces(src, g))
             for dl in range(PER):
                 field_rows(src, g * PER + dl)
             advance(g, src, arrived(z_halo[src, g]), w, sink)
+            if then is not None:
+                pl.when(g == after)(then)
 
     wait_faces(coef_faces(FIRST))
     first_z = arrived(cz_halo[FIRST])
@@ -459,30 +491,6 @@
     step(T1, Iterate(T2), cheb[2])
     step(T2, Observe(B0), cheb[3])
 
-    def sum_copy(stage, place, o):
-        return pltpu.make_async_remote_copy(
-            src_ref=sums.at[stage, place],
-            dst_ref=sums.at[stage, place],
-            send_sem=rsend_sem.at[stage, o],
-            recv_sem=rrecv_sem.at[stage, o],
-            device_id=peer(stage, o),
-            device_id_type=pl.DeviceIdType.MESH,
-        )
-
-    def sum_start(stage, value):
-        sums[stage, places[stage]] = value
-        for o in range(1, counts[stage]):
-            sum_copy(stage, places[stage], o).start()
-
-    def sum_end(stage):
-        for o in range(1, counts[stage]):
-            sum_copy(stage, lax.rem(places[stage] + counts[stage] - o, counts[stage]), o).wait_recv()
-        parts = [sums[stage, place] for place in range(counts[stage])]
-        while len(parts) > 1:
-            parts = [p + q for p, q in zip(parts[::2], parts[1::2])]
-        return parts[0]
-
-    sum_start(0, jnp.sum(partial[...], axis=1))
     step(B0, Iterate(B1), cheb[1])
     sum_start(1, sum_end(0))
     step(B1, Iterate(B2), cheb[2])
@@ -502,8 +510,14 @@
             sum_copy(stage, places[stage], o).wait_send()
 
 
-def finish(cells, sums, quo_ref):
+def finish(cells, result, sums, out_hbm, quo_ref, sem):
+    parts = [pl.ds(d, 1) for d in range(NDIR)]
+    copies = [pltpu.make_async_copy(result.at[p], out_hbm.at[p], sem.at[i]) for i, p in enumerate(parts)]
+    for copy in copies:
+        copy.start()
     quo_ref[...] = jnp.sum(sums[...], axis=1) / cells
+    for copy in copies:
+        copy.wait()
 
 
 def solution(mesh):
@@ -563,13 +577,18 @@
             log_cond.reshape(DENSE, LANES),
             obs_mask.reshape(DENSE, LANES),
         )
-        quotient = pl.pallas_call(
+        result, sums = (pltpu.with_memory_space_constraint(v, pltpu.VMEM) for v in (result, sums))
+        out, quotient = pl.pallas_call(
             lambda *refs: finish(cells, *refs),
-            out_shape=jax.ShapeDtypeStruct((NDIR,), f32),
-            in_specs=[vmem_spec],
-            out_specs=vmem_spec,
-        )(pltpu.with_memory_space_constraint(sums, pltpu.VMEM))
-        return result.reshape(directions.shape), quotient
+            out_shape=(
+                jax.ShapeDtypeStruct((NDIR, DENSE, LANES), f32),
+                jax.ShapeDtypeStruct((NDIR,), f32),
+            ),
+            in_specs=[vmem_spec, vmem_spec],
+            out_specs=(any_spec, vmem_spec),
+            scratch_shapes=[pltpu.SemaphoreType.DMA((NDIR,))],
+        )(result, sums)
+        return out.reshape(directions.shape), quotient
 
     placed = P("gx", "gy", "gz")
     stacked = P(None, "gx", "gy", "gz")

time: 48.2 us -> 47.4 us (0.983)
  local copies, waits for them, and re-layouts: 0.97 us -> 0 us
    unnamed x1 -> x0, local copies, waits for them, and re-layouts: 0.97 us -> none
    pallas_call x1, Pallas kernels: 0.59 us -> 1.54 us  [shards(): pl.pallas_call(lambda *refs: finish(cells, *refs), out_shape=(jax.ShapeDt...]
    pallas_call x1, Pallas kernels: 45.9 us -> 45.1 us  [shards(): pl.pallas_call(lambda *refs: kernel(sizes, *refs), out_shape=(pltpu.VMEM(...]
where the time goes in v3:
time: 47.4 us; the launch traced here: 47.3 us
  Pallas kernels  46.6 us (98%)
  between operations  0.64 us (1%)
    pallas_call x1, Pallas kernels, shards(): pl.pallas_call(lambda *refs: kernel(sizes, *refs), out_shape=(pltpu.VMEM(...  45.1 us
    pallas_call x1, Pallas kernels, shards(): pl.pallas_call(lambda *refs: finish(cells, *refs), out_shape=(jax.ShapeDt...  1.54 us

profile of v3, /device:TPU:8, one launch (start us, length us, event | category | flops | bytes accessed | tf_op | source)
XLA Modules:
  0.0 47.3 jit_solution(2671524787414456938)
XLA Ops:
  0.6 45.1 %shard_map.59 = (f32[8,256,128]{2,1,0:T(8,128)S(1)}, f32[8,128]{1,0:T(8,128)S(1)}) custom-call(f32[8,256,128]{2,1,0:T(8,128)} %bitcast.5, f32[256,128]{1,0:T(8,128)} %bitcast.6, f32[256,128]{1,0:T(8,128)} %bitcast.7, s32[256,128]{1,0:T(8,128)} %bitcast.8), custom_call_target="tpu_custom_call" | custom-call | tf_op jit(solution)/shard_map/pallas_call | solution.py:534
  45.7 1.5 %shard_map.60 = (f32[8,256,128]{2,1,0:T(8,128)}, f32[8]{0:T(128)}) custom-call(f32[8,256,128]{2,1,0:T(8,128)S(1)} %get-tuple-element.6.refs_0_, f32[8,128]{1,0:T(8,128)S(1)} %get-tuple-element.7.refs_1_), custom_call_target="tpu_custom_call" | custom-call | tf_op jit(solution)/shard_map/pallas_call | solution.py:581

commit v4 on v3

--- a/solution.py
+++ b/solution.py
@@ -24,7 +24,7 @@
 DELTA, T1, T2, B0, B1, B2, T0 = range(7)
 EXCHANGES = 6
 STATE, FIRST = range(2)
-GREETED = (0, 1, 2)
+GREETED = (1,)
 
 
 def chebyshev(count):

time: 47.4 us -> 47.1 us (level)
  no operation moved by 1% of the time
where the time goes in v4:
time: 47.1 us; the launch traced here: 47 us
  Pallas kernels  46.3 us (98%)
  between operations  0.64 us (1%)
    pallas_call x1, Pallas kernels, shards(): pl.pallas_call(lambda *refs: kernel(sizes, *refs), out_shape=(pltpu.VMEM(...  44.8 us
    pallas_call x1, Pallas kernels, shards(): pl.pallas_call(lambda *refs: finish(cells, *refs), out_shape=(jax.ShapeDt...  1.54 us

profile of v4, /device:TPU:8, one launch (start us, length us, event | category | flops | bytes accessed | tf_op | source)
XLA Modules:
  0.0 47.0 jit_solution(1754612309712541282)
XLA Ops:
  0.6 44.8 %shard_map.59 = (f32[8,256,128]{2,1,0:T(8,128)S(1)}, f32[8,128]{1,0:T(8,128)S(1)}) custom-call(f32[8,256,128]{2,1,0:T(8,128)} %bitcast.5, f32[256,128]{1,0:T(8,128)} %bitcast.6, f32[256,128]{1,0:T(8,128)} %bitcast.7, s32[256,128]{1,0:T(8,128)} %bitcast.8), custom_call_target="tpu_custom_call" | custom-call | tf_op jit(solution)/shard_map/pallas_call | solution.py:534
  45.4 1.5 %shard_map.60 = (f32[8,256,128]{2,1,0:T(8,128)}, f32[8]{0:T(128)}) custom-call(f32[8,256,128]{2,1,0:T(8,128)S(1)} %get-tuple-element.6.refs_0_, f32[8,128]{1,0:T(8,128)S(1)} %get-tuple-element.7.refs_1_), custom_call_target="tpu_custom_call" | custom-call | tf_op jit(solution)/shard_map/pallas_call | solution.py:581
